TPU v7x, 32 devices: a whole 2x2x4 slice. The times are simulated.
32 devices in a mesh: rows: 8 (over z, y), sub: 4 (over x, core).
Axes of the slice: x: 2, y: 2, z: 4, core: 2. Of those that a mesh axis runs over, the one named last changes fastest.
Arguments:
- snapshots: float32 [513, 32768], P(None, ('rows', 'sub')), may hold values from -6 to 6
- start: float32 [512, 64], replicated, may hold values from -6 to 6
Outputs:
- modes: float32 [128, 32768], P(None, ('rows', 'sub'))
- operator: float32 [128, 128], replicated
- coefficients: float32 [128, 513], replicated
All inputs are finite; a program needn't handle non-finite values.
Results may differ from a plain program's by a relative error of at most 0.0003.
Values sent between devices are 32-bit elements; how exact they have to be, the bound alone decides.
A program may use at most 64 MiB of HBM per device.

v0:
```python
import functools

import jax
import jax.numpy as jnp
from jax import lax
from jax.experimental import pallas as pl
from jax.experimental.pallas import tpu as pltpu
from jax.sharding import PartitionSpec as P

HIGHEST = lax.Precision.HIGHEST
TILE = 8
LANES = 128
PANEL = 4


def dot(left, right, dims):
    return lax.dot_general(
        left, right, (dims, ((), ())), precision=HIGHEST, preferred_element_type=jnp.float32
    )


def nn(left, right):
    return dot(left, right, ((1,), (0,)))


def nt(left, right):
    return dot(left, right, ((1,), (1,)))


def tn(left, right):
    return dot(left, right, ((0,), (0,)))


def iotas(rows, lanes):
    return (
        lax.broadcasted_iota(jnp.int32, (rows, lanes), 0),
        lax.broadcasted_iota(jnp.int32, (rows, lanes), 1),
    )


def eliminate(blocks, offset, width):
    tiles = [[b[t : t + TILE] for t in range(0, width, TILE)] for b in blocks]
    shape = (TILE, 2 * width)
    sub = lax.broadcasted_iota(jnp.int32, shape, 0)
    for j in range(0, width, PANEL):
        home, inner = j // TILE, j % TILE
        at = offset + j
        live = range(home, width // TILE)
        for own in tiles:
            cols = [
                {t: jnp.broadcast_to(own[t][:, at + q : at + q + 1], shape) for t in live} for q in range(PANEL)
            ]
            rows = [jnp.broadcast_to(own[home][inner + q : inner + q + 1], shape) for q in range(PANEL)]
            small = [
                [
                    jnp.broadcast_to(cols[c][home][inner + q : inner + q + 1], shape) if c >= q else None
                    for c in range(PANEL)
                ]
                for q in range(PANEL)
            ]
            for q in range(PANEL):
                inverse = 1.0 / small[q][q]
                factor = {t: cols[q][t] * inverse for t in live}
                factor[home] = jnp.where(sub > inner + q, factor[home], 0.0)
                for c in range(q + 1, PANEL):
                    ratio = small[q][c] * inverse
                    for e in range(c, PANEL):
                        small[c][e] = small[c][e] - ratio * small[q][e]
                    rows[c] = rows[c] - ratio * rows[q]
                    for t in live:
                        cols[c][t] = cols[c][t] - factor[t] * small[q][c]
                for t in live:
                    own[t] = own[t] - factor[t] * rows[q]
    row, lane = iotas(width, 2 * width)
    place = lane - offset
    inside = (place >= 0) & (place < width)
    out = []
    for own in tiles:
        whole = jnp.concatenate(own, 0)
        pivot = jnp.sum(jnp.where(place == row, whole, 0.0), axis=1, keepdims=True)
        whole = whole * (1.0 / jnp.sqrt(pivot))
        out.append(jnp.where(inside & (place < row), 0.0, whole))
    return out


def plan(past):
    blocks = [(r, c) for r in range(past // LANES) for c in range(r, past // LANES)]
    tails = list(range(past // LANES + 1))
    cut = (len(blocks) + 1) // 2
    keep = len(tails) - 1
    lengths = (cut * LANES + keep * TILE, (len(blocks) - cut) * LANES + TILE)
    half = -(-max(lengths) // (4 * TILE)) * 4 * TILE
    where = {}
    for n, block in enumerate(blocks):
        where[block] = n * LANES if n < cut else half + (n - cut) * LANES
    tail_rows = [cut * LANES + TILE * c for c in range(keep)] + [half + (len(blocks) - cut) * LANES]
    return half, where, tail_rows


def split(block):
    high = block.astype(jnp.bfloat16)
    return high, (block - high.astype(jnp.float32)).astype(jnp.bfloat16)


def fast_nt(left, right, dims=((1,), (1,))):
    def one(a, b):
        return lax.dot_general(a, b, (dims, ((), ())), preferred_element_type=jnp.float32)

    return one(left[0], right[0]) + (one(left[0], right[1]) + one(left[1], right[0]))


def gram_kernel(sizes, snap_ref, start_ref, out_ref, right_ref, acc, full, got0, got1, got2, got3, send_sems, recv_sems):
    rows_total, sub_total = sizes
    count = snap_ref.shape[0]
    past = count - 1
    half, where, tail_rows = plan(past)
    row, sub = lax.axis_index("rows"), lax.axis_index("sub")

    def bit(index, k):
        return lax.rem(index // (1 << k), 2)

    def step(index, k):
        return (1 - 2 * bit(index, k)) * (1 << k)

    core = bit(sub, 0)
    bx, by = bit(sub, 1), bit(row, 0)
    dx, dy = step(sub, 1), step(row, 0)
    other = 1 - core
    halvings = [
        ((row, sub + step(sub, 0)), core),
        ((row + core * dy, sub + other * dx), other * bx + core * by),
        ((row + other * dy, sub + core * dx), core * bx + other * by),
    ]
    whole = [(row, sub + step(sub, k)) for k in range(2, sub_total.bit_length() - 1)]
    whole += [(row + step(row, k), sub) for k in range(1, rows_total.bit_length() - 1)]
    partners = [h[0] for h in halvings] + whole

    barrier = pltpu.get_barrier_semaphore()
    for partner in partners:
        pl.semaphore_signal(barrier, inc=1, device_id=partner, device_id_type=pl.DeviceIdType.MESH)

    for (r, c), place in where.items():
        if r == c:
            panel = fast_nt(split(snap_ref[r * LANES : (r + 1) * LANES]), split(snap_ref[r * LANES : past]))
        acc[place : place + LANES] = panel[:, (c - r) * LANES : (c - r + 1) * LANES]
    last = jnp.concatenate([snap_ref[past:count], jnp.zeros((TILE - 1, snap_ref.shape[1]), jnp.float32)], 0)
    tail = fast_nt(split(last), split(snap_ref[:past]))
    for c, place in enumerate(tail_rows[:-1]):
        acc[place : place + TILE] = tail[:, c * LANES : (c + 1) * LANES]
    corner = jnp.sum(last * last, axis=1, keepdims=True)
    lane = lax.broadcasted_iota(jnp.int32, (TILE, LANES), 1)
    acc[tail_rows[-1] : tail_rows[-1] + TILE] = jnp.where(lane == 0, corner, 0.0)
    end0, end1 = tail_rows[-2] + TILE, tail_rows[-1] + TILE
    if end0 < half:
        acc[end0:half] = jnp.zeros((half - end0, LANES), jnp.float32)
    if end1 < 2 * half:
        acc[end1 : 2 * half] = jnp.zeros((2 * half - end1, LANES), jnp.float32)

    pl.semaphore_wait(barrier, len(partners))

    def orthonormal():
        start = start_ref[...]
        width = start_ref.shape[0]
        eye_row, eye_lane = iotas(width, 2 * width)
        eye_right = (eye_lane - width == eye_row).astype(jnp.float32)
        block = jnp.where(eye_lane < width, nt(start, twice(start)), eye_right)
        (first,) = eliminate([block], 0, width)
        right_ref[...] = dot(start, twice(first[:, width:]), ((0,), (1,)))

    def exchange(n, src, dst, partner, beside=None):
        copy = pltpu.make_async_remote_copy(
            src_ref=src,
            dst_ref=dst,
            send_sem=send_sems.at[n],
            recv_sem=recv_sems.at[n],
            device_id=partner,
            device_id_type=pl.DeviceIdType.MESH,
        )
        copy.start()
        if beside is not None:
            beside()
        copy.wait()

    def rows_at(start, length):
        return pl.ds(pl.multiple_of(start, TILE), length)

    offset, length, n = 0, half, 0
    trail = []
    for (partner, side), got in zip(halvings, (got0, got1, got2)):
        beside = orthonormal if n == 0 else None
        exchange(n, acc.at[rows_at(offset + (1 - side) * length, length)], got, partner, beside)
        offset = offset + side * length
        mine = rows_at(offset, length)
        acc[mine] = acc[mine] + got[...]
        trail.append((partner, offset, length))
        length, n = length // 2, n + 1
    length = length * 2
    mine = rows_at(offset, length)
    for k, partner in enumerate(whole):
        exchange(n, acc.at[mine], got3.at[k], partner)
        n += 1
        target = full if k == len(whole) - 1 else acc
        target[mine] = acc[mine] + got3[k]
    for partner, begin, span in reversed(trail):
        part = rows_at(begin, span)
        exchange(n, full.at[part], full.at[part], partner)
        n += 1
    out_ref[...] = full[...]


def unpack(packed_ref, gram_ref, past):
    _, where, tail_rows = plan(past)
    gram_ref[past:] = jnp.zeros((gram_ref.shape[0] - past, gram_ref.shape[1]), jnp.float32)
    for (r, c), place in where.items():
        block = packed_ref[place : place + LANES]
        gram_ref[r * LANES : (r + 1) * LANES, c * LANES : (c + 1) * LANES] = block
        if r != c:
            gram_ref[c * LANES : (c + 1) * LANES, r * LANES : (r + 1) * LANES] = block.T
    extra = gram_ref.shape[1] - past
    lane = lax.broadcasted_iota(jnp.int32, (LANES, extra), 1)
    for c, place in enumerate(tail_rows):
        block = packed_ref[place : place + TILE]
        if c * LANES < past:
            gram_ref[past : past + TILE, c * LANES : (c + 1) * LANES] = block
            column = jnp.concatenate([block, jnp.zeros((LANES - TILE, LANES), jnp.float32)], 0).T
            gram_ref[c * LANES : (c + 1) * LANES, past:] = jnp.where(lane == 0, column[:, :extra], 0.0)
        else:
            gram_ref[past : past + TILE, past:] = block[:, :extra]


def twice(block):
    return jnp.concatenate([block, block], 0)


def chain_kernel(total_cells, snap_ref, packed_ref, right_ref, modes_ref, operator_ref, coef_ref, z_ref, gram_ref):
    past, order = right_ref.shape
    width = order // 2
    count = past + 1
    padded = gram_ref.shape[0]
    unpack(packed_ref, gram_ref, past)
    row, lane = iotas(width, order)
    low = lane < width
    eye_left = (lane == row).astype(jnp.float32)
    eye_right = (lane - width == row).astype(jnp.float32)

    def lows(rows):
        return lax.broadcasted_iota(jnp.int32, (rows, order), 1) < width

    def shift(block):
        z_ref[...] = jnp.zeros_like(z_ref)
        z_ref[1 : past + 1] = block
        return z_ref[...]

    def pad(block):
        return jnp.concatenate([block, jnp.zeros((padded - past, order), jnp.float32)], 0)

    right = right_ref[...]
    rp, rs = pad(right), shift(right)
    pair = jnp.concatenate([rp, rs], 1)
    gram = split(gram_ref[...])
    gpair = fast_nt(gram, split(pair), ((1,), (0,)))
    image_gram = tn(right, gpair[:past, :order])
    adv_gram = tn(rs, gpair[:, order:])
    residual = gpair[:past, :order] - nn(jnp.where(lows(past), right, 0.0), image_gram)
    m1, h1 = eliminate(
        [jnp.where(low, image_gram[:width], eye_right), jnp.where(low, adv_gram[:width], eye_right)], 0, width
    )
    second = nt(jnp.where(lows(past), 0.0, residual), twice(m1))
    basis = jnp.where(lows(past), right, second)
    zp, zs = pad(basis), shift(basis)
    zpair = jnp.concatenate([zp, zs], 1)
    gz = fast_nt(gram, split(zpair), ((1,), (0,)))
    prods = tn(zpair, gz)
    kmat, fmat, hmat = prods[:order, :order], prods[:order, order:], prods[order:, order:]

    def reduce_first(first, mat):
        rolled = pltpu.roll(first, width, 1)
        n1 = jnp.concatenate([jnp.where(low, rolled, 0.0), eye_right], 0)
        mid = nt(nn(n1, mat), n1)
        couple = jnp.where(low, 0.0, mid[:width])
        corner = mid[width:] - tn(couple, couple)[width:]
        tail = nn(jnp.where(low, -mid[width:], eye_right), n1)
        return n1, couple, jnp.where(low, eye_left, corner), tail

    kn1, kcouple, kcorner, ktail = reduce_first(m1, kmat)
    hn1, _, hcorner, htail = reduce_first(h1, hmat)
    m2, h2 = eliminate([kcorner, hcorner], width, width)
    ninv = jnp.concatenate([kn1[:width], nn(m2[:, :width], ktail)], 0)
    hinv = jnp.concatenate([hn1[:width], nn(h2[:, :width], htail)], 0)
    triangle = jnp.concatenate([jnp.where(low, m1, kcouple), jnp.where(low, 0.0, m2)], 0)

    operator_ref[...] = nt(nn(ninv, fmat), ninv)
    scale = jnp.sqrt(jnp.asarray(total_cells, jnp.float32))
    solver = nn(nt(triangle, hinv), hinv) * (1.0 / scale)
    coef_ref[...] = nt(gz[:, order:], solver)[:count]
    weights = nt(ninv, zs) * scale
    bulk = fast_nt(split(weights[:, :past]), split(snap_ref[:past]), ((1,), (0,)))
    modes_ref[...] = bulk + weights[:, past:count] * snap_ref[past:count]


def shards(sizes, snapshots, start):
    count, cells = snapshots.shape
    past, width = start.shape
    order = 2 * width
    padded = -(-count // TILE) * TILE
    vmem = pl.BlockSpec(memory_space=pltpu.VMEM)
    half, _, _ = plan(past)
    copies = (sizes[0] * sizes[1]).bit_length() - 1
    packed, right = pl.pallas_call(
        functools.partial(gram_kernel, sizes),
        out_shape=(
            jax.ShapeDtypeStruct((2 * half, LANES), jnp.float32),
            jax.ShapeDtypeStruct((past, order), jnp.float32),
        ),
        in_specs=[vmem] * 2,
        out_specs=(vmem,) * 2,
        scratch_shapes=[
            pltpu.VMEM((2 * half, LANES), jnp.float32),
            pltpu.VMEM((2 * half, LANES), jnp.float32),
            pltpu.VMEM((half, LANES), jnp.float32),
            pltpu.VMEM((half // 2, LANES), jnp.float32),
            pltpu.VMEM((half // 4, LANES), jnp.float32),
            pltpu.VMEM((copies - 3, half // 4, LANES), jnp.float32),
            pltpu.SemaphoreType.DMA((copies + 3,)),
            pltpu.SemaphoreType.DMA((copies + 3,)),
        ],
        compiler_params=pltpu.CompilerParams(
            collective_id=0, has_side_effects=True, vmem_limit_bytes=60 << 20
        ),
        name="gram",
    )(snapshots, start.T)
    modes, operator, coefficients = pl.pallas_call(
        functools.partial(chain_kernel, cells * sizes[0] * sizes[1]),
        out_shape=(
            jax.ShapeDtypeStruct((order, cells), jnp.float32),
            jax.ShapeDtypeStruct((order, order), jnp.float32),
            jax.ShapeDtypeStruct((count, order), jnp.float32),
        ),
        in_specs=[vmem] * 3,
        out_specs=(vmem,) * 3,
        scratch_shapes=[pltpu.VMEM((padded, order), jnp.float32), pltpu.VMEM((padded, padded), jnp.float32)],
        compiler_params=pltpu.CompilerParams(vmem_limit_bytes=60 << 20),
        name="chain",
    )(snapshots, packed, right)
    return modes, operator, coefficients.T


def solution(mesh):
    def body(snapshots, start):
        return shards((mesh.shape["rows"], mesh.shape["sub"]), snapshots, start)

    return jax.shard_map(
        body,
        mesh=mesh,
        in_specs=(P(None, ("rows", "sub")), P()),
        out_specs=(P(None, ("rows", "sub")), P(), P()),
        check_vma=False,
    )
```

profile of v0, /device:TPU:0, one launch (start us, length us, event | category | flops | bytes accessed | tf_op | source)
XLA Modules:
  0.0 58.7 jit_solution(11836258020390884686)
XLA Ops:
  0.6 39.5 %gram.1 = (f32[1344,128]{1,0:T(8,128)}, f32[512,128]{1,0:T(8,128)}) custom-call(f32[513,1024]{1,0:T(8,128)} %snap_ref.3, f32[64,512]{1,0:T(8,128)} %bitcast.2), custom_call_target="tpu_custom_call" | custom-call | tf_op jit(solution)/shard_map/gram/pallas_call | solution.py:309
  40.2 18.5 %chain.1 = (f32[128,1024]{1,0:T(8,128)}, f32[128,128]{1,0:T(8,128)}, f32[513,128]{1,0:T(8,128)}) custom-call(f32[513,1024]{1,0:T(8,128)} %snap_ref.3, f32[1344,128]{1,0:T(8,128)} %get-tuple-element.8.packed_ref, f32[512,128]{1,0:T(8,128)} %get-tuple-element.9.right_ref), custom_call_target="tpu_custom_call" | custom-call | tf_op jit(solution)/shard_map/chain/pallas_call | solution.py:332
where the time goes:
time: 58.9 us; the launch traced here: 58.7 us
  Pallas kernels  58.1 us (99%)
  between operations  0.64 us (1%)
    pallas_call x1, Pallas kernels, shards(): pl.pallas_call(functools.partial(gram_kernel, sizes), out_shape=(jax.Shap...  39.5 us
    pallas_call x1, Pallas kernels, shards(): pl.pallas_call(functools.partial(chain_kernel, cells * sizes[0] * sizes[1...  18.5 us

commit v1 on v0

--- a/solution.py
+++ b/solution.py
@@ -187,7 +187,7 @@
     offset, length, n = 0, half, 0
     trail = []
     for (partner, side), got in zip(halvings, (got0, got1, got2)):
-        beside = orthonormal if n == 0 else None
+        beside = None
         exchange(n, acc.at[rows_at(offset + (1 - side) * length, length)], got, partner, beside)
         offset = offset + side * length
         mine = rows_at(offset, length)
@@ -197,7 +197,7 @@
     length = length * 2
     mine = rows_at(offset, length)
     for k, partner in enumerate(whole):
-        exchange(n, acc.at[mine], got3.at[k], partner)
+        exchange(n, acc.at[mine], got3.at[k], partner, orthonormal if k == len(whole) - 1 else None)
         n += 1
         target = full if k == len(whole) - 1 else acc
         target[mine] = acc[mine] + got3[k]
@@ -325,7 +325,7 @@
             pltpu.SemaphoreType.DMA((copies + 3,)),
         ],
         compiler_params=pltpu.CompilerParams(
-            collective_id=0, has_side_effects=True, vmem_limit_bytes=60 << 20
+            collective_id=0, has_side_effects=True, vmem_limit_bytes=16 << 20
         ),
         name="gram",
     )(snapshots, start.T)
@@ -339,7 +339,7 @@
         in_specs=[vmem] * 3,
         out_specs=(vmem,) * 3,
         scratch_shapes=[pltpu.VMEM((padded, order), jnp.float32), pltpu.VMEM((padded, padded), jnp.float32)],
-        compiler_params=pltpu.CompilerParams(vmem_limit_bytes=60 << 20),
+        compiler_params=pltpu.CompilerParams(vmem_limit_bytes=20 << 20),
         name="chain",
     )(snapshots, packed, right)
     return modes, operator, coefficients.T

time: 58.9 us -> 54.7 us (0.929)
  Pallas kernels: 58.1 us -> 51.3 us
  local copies, waits for them, and re-layouts: 0 us -> 2.5 us
    pallas_call x1, Pallas kernels: 39.5 us -> 34.6 us  [shards(): pl.pallas_call(functools.partial(gram_kernel, sizes), out_shape=(jax.Shap...]
    unnamed x0 -> x6, local copies, waits for them, and re-layouts: none -> 2.5 us
    pallas_call x1, Pallas kernels: 18.5 us -> 16.7 us  [shards(): pl.pallas_call(functools.partial(chain_kernel, cells * sizes[0] * sizes[1...]
where the time goes in v1:
time: 54.7 us; the launch traced here: 54.5 us
  Pallas kernels  51.3 us (94%)
  local copies, waits for them, and re-layouts  2.5 us (5%)
  between operations  0.66 us (1%)
    pallas_call x1, Pallas kernels, shards(): pl.pallas_call(functools.partial(gram_kernel, sizes), out_shape=(jax.Shap...  34.6 us
    pallas_call x1, Pallas kernels, shards(): pl.pallas_call(functools.partial(chain_kernel, cells * sizes[0] * sizes[1...  16.7 us
    unnamed x6, local copies, waits for them, and re-layouts  2.5 us

profile of v1, /device:TPU:0, one launch (start us, length us, event | category | flops | bytes accessed | tf_op | source)
XLA Modules:
  0.0 54.5 jit_solution(927225282502280017)
XLA Ops:
  0.6 0.0 copy-start
  0.6 1.6 %copy-done = f32[513,1024]{1,0:T(8,128)S(1)} copy-done((f32[513,1024]{1,0:T(8,128)S(1)}, f32[513,1024]{1,0:T(8,128)}, u32[]{:S(2)}) %copy-start) | copy-done | bytes 2101272
  2.2 0.0 copy-start.2
  2.2 0.9 %copy-done.2 = f32[512,64]{0,1:T(8,128)S(1)} copy-done((f32[512,64]{0,1:T(8,128)S(1)}, f32[512,64]{0,1:T(8,128)}, u32[]{:S(2)}) %copy-start.2) | copy-done | bytes 131096
  3.1 0.0 copy-start.1
  3.1 34.6 %gram.1 = (f32[1344,128]{1,0:T(8,128)S(1)}, f32[512,128]{1,0:T(8,128)S(1)}) custom-call(f32[513,1024]{1,0:T(8,128)S(1)} %copy-done, f32[64,512]{1,0:T(8,128)S(1)} %bitcast.2), custom_call_target="tpu_custom_call" | custom-call | tf_op jit(solution)/shard_map/gram/pallas_call | solution.py:309
  37.8 0.0 copy-done.1
  37.8 16.7 %chain.1 = (f32[128,1024]{1,0:T(8,128)}, f32[128,128]{1,0:T(8,128)}, f32[513,128]{1,0:T(8,128)}) custom-call(f32[513,1024]{1,0:T(8,128)S(1)} %copy-done.1, f32[1344,128]{1,0:T(8,128)S(1)} %get-tuple-element.8.packed_ref, f32[512,128]{1,0:T(8,128)S(1)} %get-tuple-element.9.right_ref), custom_call_target="tpu_custom_call" | custom-call | tf_op jit(solution)/shard_map/chain/pallas_call | solution.py:332
Async XLA Ops:
  0.6 1.6 %copy-start = (f32[513,1024]{1,0:T(8,128)S(1)}, f32[513,1024]{1,0:T(8,128)}, u32[]{:S(2)}) copy-start(f32[513,1024]{1,0:T(8,128)} %snap_ref.3) | copy-start | bytes 6303748
  2.2 0.9 %copy-start.2 = (f32[512,64]{0,1:T(8,128)S(1)}, f32[512,64]{0,1:T(8,128)}, u32[]{:S(2)}) copy-start(f32[512,64]{0,1:T(8,128)} %param.3) | copy-start | bytes 393220
  3.1 34.7 %copy-start.1 = (f32[513,1024]{1,0:T(8,128)S(1)}, f32[513,1024]{1,0:T(8,128)}, u32[]{:S(2)}) copy-start(f32[513,1024]{1,0:T(8,128)} %snap_ref.3) | copy-start | bytes 6303748
